TPU v7x, 32 devices: a whole 2x2x4 slice. The times are simulated.
32 devices in a mesh: dp: 8 (over z, x), var: 4 (over y, core).
Axes of the slice: x: 2, y: 2, z: 4, core: 2. Of those that a mesh axis runs over, the one named last changes fastest.
Arguments:
- pixels: bfloat16 [8, 24, 4, 256], P('dp', 'var'), may hold values from -6 to 6
- var_ids: int32 [8, 24], P('dp', 'var'), may hold values from 0 to 90, as said below
- counts: int32 [8], P('dp'), may hold values from 3 to 24, as said below
- patch_weight: bfloat16 [91, 4, 1024], replicated, may hold values from -3 to 3
- var_embed: bfloat16 [91, 1024], replicated, may hold values from -5 to 5
- norm_gain: float32 [1024], replicated, may hold values from 0.1 to 1.9
- norm_bias: float32 [1024], replicated, may hold values from -3 to 3
- key_weight: bfloat16 [1024, 1024], P('dp'), may hold values from -0.1875 to 0.1875
- value_weight: bfloat16 [1024, 1024], P('dp'), may hold values from -0.1875 to 0.1875
- query: float32 [16, 64], replicated, may hold values from -200 to 200
- out_weight: bfloat16 [1024, 1024], replicated, may hold values from -0.1875 to 0.1875
Outputs:
- aggregated: bfloat16 [8, 256, 1024], P('dp', 'var')
Inputs may be any that keep to these rules, and one draw needn't show every extreme that they name: `var_ids`: in each sample the ids of slots below its count are distinct; slots at or past the count are padding with arbitrary ids. `counts`: some sample has exactly min(91, 24) live slots and some has exactly 3.
All inputs are finite; a program needn't handle non-finite values.
Results may differ from a plain program's by a relative error of at most 0.018.
Values may be sent and summed in bfloat16 or wider, within the bound.
A program may use at most 64 MiB of HBM per device.

v0:
```python
import math
import jax
import jax.numpy as jnp
from jax import lax
from jax.sharding import PartitionSpec as P


def on_device(
    pixels,
    var_ids,
    counts,
    patch_weight,
    var_embed,
    norm_gain,
    norm_bias,
    key_weight,
    value_weight,
    query,
    out_weight,
):
    slots = pixels.shape[1]
    patches = pixels.shape[3]
    width = out_weight.shape[0]
    heads = query.shape[0]
    head_size = query.shape[1]
    ids = var_ids[0]
    table = patch_weight[ids]
    embedded = jnp.einsum("skp,skd->spd", pixels[0], table, preferred_element_type=jnp.float32)
    embedded = embedded + var_embed[ids].astype(jnp.float32)[:, None, :]
    center = embedded - jnp.mean(embedded, axis=-1, keepdims=True)
    spread = jnp.mean(center * center, axis=-1, keepdims=True)
    normed = (center * lax.rsqrt(spread + 1e-05) * norm_gain + norm_bias).astype(jnp.bfloat16)
    flat = normed.reshape(slots * patches, width)
    local_fold = jnp.einsum(
        "jhe,he->jh",
        key_weight.astype(jnp.float32).reshape(-1, heads, head_size),
        query,
        precision=lax.Precision.HIGHEST,
    )
    folded = lax.all_gather(local_fold, "dp", axis=0, tiled=True)
    values = jnp.dot(
        flat,
        lax.all_gather(value_weight, "dp", axis=0, tiled=True),
        preferred_element_type=jnp.float32,
    )
    scores = jnp.dot(flat.astype(jnp.float32), folded, precision=lax.Precision.HIGHEST)
    scores = (scores * (1.0 / math.sqrt(head_size))).reshape(slots, patches, heads)
    first_slot = lax.axis_index("var") * slots
    live = (first_slot + jnp.arange(slots, dtype=jnp.int32) < counts[0])[:, None, None]
    scores = jnp.where(live, scores, jnp.float32(-1e30))
    values = values.astype(jnp.bfloat16).reshape(slots, patches, width)
    values_all = lax.all_to_all(values, "var", split_axis=1, concat_axis=0, tiled=True)
    scores_all = lax.all_to_all(scores, "var", split_axis=1, concat_axis=0, tiled=True)
    owned = scores_all.shape[1]
    peak = jnp.max(scores_all, axis=0)
    expo = jnp.exp(scores_all - peak)
    total = jnp.sum(expo, axis=0)
    numer = jnp.einsum(
        "sph,sphe->phe",
        expo.astype(jnp.bfloat16),
        values_all.reshape(-1, owned, heads, head_size),
        preferred_element_type=jnp.float32,
    )
    mixed = (numer / total[:, :, None]).reshape(-1, width).astype(jnp.bfloat16)
    return jnp.dot(mixed, out_weight, preferred_element_type=jnp.float32).astype(jnp.bfloat16)[None]


def solution(mesh):
    placed = (
        P("dp", "var", None, None),
        P("dp", "var"),
        P("dp"),
        P(),
        P(),
        P(),
        P(),
        P("dp", None),
        P("dp", None),
        P(),
        P(),
    )
    return jax.shard_map(
        on_device, mesh=mesh, in_specs=placed, out_specs=P("dp", "var", None), check_vma=False
    )
```

profile of v0, /device:TPU:0, one launch (start us, length us, event | category | flops | bytes accessed | tf_op | source)
XLA Modules:
  0.0 155.5 jit_solution(17821916475907785103)
XLA Ops:
  6.5 0.0 copy-start
  6.5 0.0 all-gather.2.cloned.1.call-start
  6.5 0.7 all-gather.2.cloned.1.call-update
  7.3 0.7 fusion.7
  7.9 1.5 gather_fusion.1
  9.5 1.7 %gather_fusion = bf16[6,4,1024]{2,1,0:T(4,128)(2,1)S(1)} fusion(bf16[91,4,1024]{2,1,0:T(4,128)(2,1)} %param.14, s32[1024]{0:T(1024)S(1)} %pad_clamp_fusion), kind=kCustom, calls=%fused_computation | custom fusion | bytes 98328 | tf_op jit(solution)/shard_map/gather | solution.py:27
  11.2 1.1 copy.28
  12.3 1.0 fusion.8
  13.3 32.6 %all_gather.6 = f32[1024,16]{0,1:T(8,128)S(1)} all-gather(f32[128,16]{0,1:T(8,128)S(1)} %bitcast.71), channel_id=1, replica_groups=mesh['dp'=8,'var'=4] {'dp'}, dimensions={0}, use_global_device_ids=true | all-gather | bytes 73728 | tf_op jit(solution)/shard_map/all_gather | solution.py:40
  45.9 0.0 copy-start.2
  46.0 0.0 copy-start.3
  46.0 1.8 %bitcast_reduce_fusion = (f32[6,256]{1,0:T(8,128)S(1)}, f32[6,1024,256]{1,2,0:T(8,128)S(1)}) fusion(f32[6,1024]{1,0:T(8,128)S(1)} %convert_element_type.27, bf16[6,4,1024]{2,1,0:T(4,128)(2,1)S(1)} %gather_fusion, bf16[1,6,4,256]{3,2,1,0:T(4,128)(2,1)} %param.11), kind=kOutput, calls=%fused_computation.3 | convolution fusion | flops 15727104 | bytes 6383616 | tf_op jit(solution)/shard_map/skp,skd->spd/dot_general | solution.py:28
  47.8 1.0 multiply_reduce_fusion
  48.8 0.0 copy-done.2
  48.8 0.0 copy-done.3
  48.8 1.4 add_convert_fusion
  50.2 0.0 copy-start.1
  50.2 1.7 %copy-done.1 = bf16[6,256,1024]{2,1,0:T(8,128)(2,1)} copy-done((bf16[6,256,1024]{2,1,0:T(8,128)(2,1)}, bf16[6,256,1024]{2,1,0:T(8,128)(2,1)S(1)}, u32[]{:S(2)}) %copy-start.1) | copy-done | bytes 3145752
  51.9 2.5 %convolution_multiply_fusion = f32[1536,16]{0,1:T(8,128)S(1)} fusion(bf16[1536,1024]{1,0:T(8,128)(2,1)S(1)} %bitcast.62, f32[1024,16]{0,1:T(8,128)S(1)} %all_gather.6), kind=kOutput, calls=%fused_computation.9 | convolution fusion | flops 302014464 | bytes 3309568 | tf_op jit(solution)/shard_map/dot_general | solution.py:46
  55.2 0.1 broadcast_select_fusion
  55.2 0.4 copy.29
  55.7 1.0 reshape.95
  56.7 3.3 %all-to-all-start = ((f32[4,1,6144]{2,1,0:T(1,128)}), f32[4,1,6144]{2,1,0:T(1,128)S(1)}, u32[]{:S(2)}, u32[]{:S(2)}) async-start(f32[4,1,6144]{2,1,0:T(1,128)} %reshape.95), calls=%async_computation | async-start | bytes 196608 | tf_op jit(solution)/shard_map/all_to_all | solution.py:53
  60.0 1.5 all-gather.2.cloned.1.call-done
  61.5 6.0 %convolution_convert_fusion = bf16[1536,1024]{1,0:T(8,128)(2,1)S(1)} fusion(bf16[1536,1024]{1,0:T(8,128)(2,1)} %bitcast.63, bf16[1024,1024]{1,0:T(8,128)(2,1)} %all-gather.2.cloned.1.call-done), kind=kOutput, calls=%fused_computation.8 | convolution fusion | flops 3222798336 | bytes 8388608 | tf_op jit(solution)/shard_map/dot_general | solution.py:41
  67.5 3.8 %copy.32 = bf16[6,256,1024]{2,0,1:T(8,128)(2,1)} copy(bf16[6,256,1024]{2,1,0:T(8,128)(2,1)S(1)} %bitcast.66) | data formatting | bytes 6291456 | tf_op jit(solution)/shard_map/reshape | solution.py:51
  71.2 0.0 all-to-all-done
  71.2 5.0 %all-to-all-start.1 = ((bf16[6,256,1024]{2,0,1:T(8,128)(2,1)}), bf16[6,256,1024]{2,0,1:T(8,128)(2,1)}, u32[]{:S(2)}, u32[]{:S(2)}) async-start(bf16[6,256,1024]{2,0,1:T(8,128)(2,1)} %copy.32), calls=%async_computation.1 | async-start | bytes 8388608 | tf_op jit(solution)/shard_map/all_to_all | solution.py:52
  76.3 0.5 broadcast.67
  76.8 0.9 reduce.2
  77.7 0.5 reshape.96
  78.2 0.3 copy.41
  78.5 0.1 bitcast_reduce_fusion.1
  78.6 0.5 copy.38
  79.2 0.1 exponential_reduce_fusion
  79.3 0.1 copy.35
  79.4 44.9 %all-to-all-done.1 = bf16[6,256,1024]{2,0,1:T(8,128)(2,1)} async-done(((bf16[6,256,1024]{2,0,1:T(8,128)(2,1)}), bf16[6,256,1024]{2,0,1:T(8,128)(2,1)}, u32[]{:S(2)}, u32[]{:S(2)}) %all-to-all-start.1) | async-done | bytes 3145760 | tf_op jit(solution)/shard_map/all_to_all | solution.py:52
  124.3 5.6 %copy.34 = bf16[4,6,64,1024]{3,2,1,0:T(8,128)(2,1)} copy(bf16[4,6,64,1024]{3,1,2,0:T(8,128)(2,1)} %bitcast.19) | data formatting | bytes 6291456 | tf_op jit(solution)/shard_map/all_to_all | solution.py:52
  129.9 9.2 %reshape.74 = bf16[24,64,16,64]{3,2,1,0:T(8,128)(2,1)} reshape(bf16[4,6,64,1024]{3,2,1,0:T(8,128)(2,1)} %copy.34) | data formatting | bytes 6291456 | tf_op jit(solution)/shard_map/reshape | solution.py:61
  139.1 8.0 %fusion = f32[64,16,1,64]{3,2,1,0:T(1,128)S(1)} fusion(bf16[24,64,16,1]{0,3,2,1:T(2,128)(2,1)S(1)} %copy.38, bf16[24,64,16,64]{3,2,1,0:T(8,128)(2,1)} %reshape.74), kind=kOutput, calls=%fused_computation.4 | convolution fusion | flops 3145728 | bytes 3457024 | tf_op jit(solution)/shard_map/sph,sphe->phe/dot_general | solution.py:58
  147.1 0.2 divide_convert_fusion
  147.3 0.2 convert_element_type.32
  147.5 0.0 copy-done
  147.5 1.1 fusion.2
  (8 shorter events, 0.1 us)
Async XLA Ops:
  6.5 141.0 %copy-start = (bf16[1024,1024]{1,0:T(8,128)(2,1)S(1)}, bf16[1024,1024]{1,0:T(8,128)(2,1)}, u32[]{:S(2)}) copy-start(bf16[1024,1024]{1,0:T(8,128)(2,1)} %param.21) | copy-start | bytes 6291460
  6.5 54.9 %all-gather.2.cloned.1.call-start = ((), (), s32[]{:S(2)}) async-start(), calls=%async_computation.2 | async-start | bytes 2359296 | tf_op jit(solution)/shard_map/all_gather | solution.py:43
  45.9 2.9 %copy-start.2 = (f32[1024]{0:T(1024)S(1)}, f32[1024]{0:T(1024)}, u32[]{:S(2)}) copy-start(f32[1024]{0:T(1024)} %param.17) | copy-start | bytes 12292
  46.0 2.9 %copy-start.3 = (f32[1024]{0:T(1024)S(1)}, f32[1024]{0:T(1024)}, u32[]{:S(2)}) copy-start(f32[1024]{0:T(1024)} %param.16) | copy-start | bytes 12292
  50.2 1.7 %copy-start.1 = (bf16[6,256,1024]{2,1,0:T(8,128)(2,1)}, bf16[6,256,1024]{2,1,0:T(8,128)(2,1)S(1)}, u32[]{:S(2)}) copy-start(bf16[6,256,1024]{2,1,0:T(8,128)(2,1)S(1)} %add_convert_fusion) | copy-start | bytes 9437188
  56.7 14.5 %all-to-all-start = ((f32[4,1,6144]{2,1,0:T(1,128)}), f32[4,1,6144]{2,1,0:T(1,128)S(1)}, u32[]{:S(2)}, u32[]{:S(2)}) async-start(f32[4,1,6144]{2,1,0:T(1,128)} %reshape.95), calls=%async_computation | async-start | bytes 196608 | tf_op jit(solution)/shard_map/all_to_all | solution.py:53
  71.2 53.1 %all-to-all-start.1 = ((bf16[6,256,1024]{2,0,1:T(8,128)(2,1)}), bf16[6,256,1024]{2,0,1:T(8,128)(2,1)}, u32[]{:S(2)}, u32[]{:S(2)}) async-start(bf16[6,256,1024]{2,0,1:T(8,128)(2,1)} %copy.32), calls=%async_computation.1 | async-start | bytes 8388608 | tf_op jit(solution)/shard_map/all_to_all | solution.py:52
Sparse Core Ops, SparseCore 0:
  9.5 51.9 all-gather.1
where the time goes:
time: 156 us; the launch traced here: 155 us
  waiting for transfers between devices  47.1 us (30%)
  blocking collectives  32.6 us (21%)
  local copies, waits for them, and re-layouts  28.3 us (18%)
  matrix products  20.4 us (13%)
  between operations  14.2 us (9%)
  starting transfers between devices  8.35 us (5%)
  other arithmetic  4.48 us (3%)
    all_to_all x1, waiting for transfers between devices, on_device(): lax.all_to_all(values, 'var', split_axis=1, concat_axis=0, tiled=True)  44.9 us
    all_gather x1, blocking collectives, on_device(): folded = lax.all_gather(local_fold, 'dp', axis=0, tiled=True)  32.6 us
    reshape x1, local copies, waits for them, and re-layouts, on_device(): values_all.reshape(-1, owned, heads, head_size)  9.19 us
    dot_general x1, matrix products, on_device(): jnp.einsum('sph,sphe->phe', expo.astype(jnp.bfloat16), values_all.reshape...  7.95 us
    dot_general x1, matrix products, on_device(): jnp.dot(flat, lax.all_gather(value_weight, 'dp', axis=0, tiled=True), pre...  5.98 us
    all_to_all x1, local copies, waits for them, and re-layouts, on_device(): lax.all_to_all(values, 'var', split_axis=1, concat_axis=0, tiled=True)  5.62 us
    all_to_all x1, starting transfers between devices, on_device(): lax.all_to_all(values, 'var', split_axis=1, concat_axis=0, tiled=True)  5.04 us
    unnamed x11, local copies, waits for them, and re-layouts  4.28 us
  transfers between devices with their start and end apart: 3, of which 2 were waited for; matrix products, arithmetic and copies ran while one was open for 17% of the time, Pallas kernels for 0%

commit v1 on v0

--- a/solution.py
+++ b/solution.py
@@ -49,7 +49,16 @@
     live = (first_slot + jnp.arange(slots, dtype=jnp.int32) < counts[0])[:, None, None]
     scores = jnp.where(live, scores, jnp.float32(-1e30))
     values = values.astype(jnp.bfloat16).reshape(slots, patches, width)
-    values_all = lax.all_to_all(values, "var", split_axis=1, concat_axis=0, tiled=True)
+
+    def perform_sheet_on(m):
+        return jnp.concatenate(
+            lax.all_to_all(
+                jnp.stack(jnp.split(m, lax.axis_size("var"), axis=1), axis=0), "var", 0, 0
+            ),
+            axis=0,
+        )
+
+    values_all = perform_sheet_on(values)
     scores_all = lax.all_to_all(scores, "var", split_axis=1, concat_axis=0, tiled=True)
     owned = scores_all.shape[1]
     peak = jnp.max(scores_all, axis=0)

time: 156 us -> 138 us (0.88)
  waiting for transfers between devices: 47.1 us -> 35.9 us
  local copies, waits for them, and re-layouts: 28.3 us -> 19.2 us
  other arithmetic: 4.48 us -> 6.38 us
    reshape x2 -> x0, local copies, waits for them, and re-layouts: 13 us -> none  [the longest x1 9.19 us: on_device(): values_all.reshape(-1, owned, heads, head_size)]
    all_to_all x1, waiting for transfers between devices: 44.9 us -> 33.7 us  [perform_sheet_on(): lax.all_to_all(jnp.stack(jnp.split(m, lax.axis_size('var'), axis=1), axis...]
    another operation x0 -> x2, local copies, waits for them, and re-layouts: none -> 9.5 us  [the longest x1 9.19 us: on_device(): values_all.reshape(-1, owned, heads, head_size)]
    all_to_all x1 -> x0, local copies, waits for them, and re-layouts: 5.62 us -> none  [on_device(): lax.all_to_all(values, 'var', split_axis=1, concat_axis=0, tiled=True)]
    another operation x0 -> x1, other arithmetic: none -> 1.89 us  [perform_sheet_on(): jnp.stack(jnp.split(m, lax.axis_size('var'), axis=1), axis=0)]
  transfers between devices with their start and end apart: 3 -> 3, of which waited for: 2 -> 2; matrix products, arithmetic and copies ran while one was open for 17% -> 19% of each run, Pallas kernels for 0% -> 0%
where the time goes in v1:
time: 138 us; the launch traced here: 137 us
  waiting for transfers between devices  35.9 us (26%)
  blocking collectives  32.6 us (24%)
  matrix products  20.4 us (15%)
  local copies, waits for them, and re-layouts  19.2 us (14%)
  between operations  14.3 us (10%)
  starting transfers between devices  8.14 us (6%)
  other arithmetic  6.38 us (5%)
    all_to_all x1, waiting for transfers between devices, perform_sheet_on(): lax.all_to_all(jnp.stack(jnp.split(m, lax.axis_size('var'), axis=1), axis...  33.7 us
    all_gather x1, blocking collectives, on_device(): folded = lax.all_gather(local_fold, 'dp', axis=0, tiled=True)  32.6 us
    another operation x1, local copies, waits for them, and re-layouts, on_device(): values_all.reshape(-1, owned, heads, head_size)  9.19 us
    dot_general x1, matrix products, on_device(): jnp.einsum('sph,sphe->phe', expo.astype(jnp.bfloat16), values_all.reshape...  7.95 us
    dot_general x1, matrix products, on_device(): jnp.dot(flat, lax.all_gather(value_weight, 'dp', axis=0, tiled=True), pre...  5.98 us
    all_to_all x1, starting transfers between devices, perform_sheet_on(): lax.all_to_all(jnp.stack(jnp.split(m, lax.axis_size('var'), axis=1), axis...  4.83 us
    unnamed x11, local copies, waits for them, and re-layouts  4.29 us
    all_to_all x1, starting transfers between devices, on_device(): lax.all_to_all(scores, 'var', split_axis=1, concat_axis=0, tiled=True)  3.3 us
  transfers between devices with their start and end apart: 3, of which 2 were waited for; matrix products, arithmetic and copies ran while one was open for 19% of the time, Pallas kernels for 0%

profile of v1, /device:TPU:0, one launch (start us, length us, event | category | flops | bytes accessed | tf_op | source)
XLA Modules:
  0.0 136.9 jit_solution(1398388512857979157)
XLA Ops:
  6.5 0.0 copy-start
  6.5 0.0 all-gather.2.cloned.1.call-start
  6.5 0.7 all-gather.2.cloned.1.call-update
  7.3 0.7 fusion.7
  7.9 1.5 %gather_fusion.1 = bf16[6,1024]{1,0:T(8,128)(2,1)S(1)} fusion(bf16[91,1024]{1,0:T(8,128)(2,1)} %param.15, s32[1024]{0:T(1024)S(1)} %pad_clamp_fusion), kind=kCustom, calls=%fused_computation.1 | custom fusion | bytes 24600 | tf_op jit(solution)/shard_map/gather | solution.py:29
  9.5 1.7 %gather_fusion = bf16[6,4,1024]{2,1,0:T(4,128)(2,1)S(1)} fusion(bf16[91,4,1024]{2,1,0:T(4,128)(2,1)} %param.14, s32[1024]{0:T(1024)S(1)} %pad_clamp_fusion), kind=kCustom, calls=%fused_computation | custom fusion | bytes 98328 | tf_op jit(solution)/shard_map/gather | solution.py:27
  11.2 1.1 copy.21
  12.3 1.0 fusion.8
  13.3 32.6 %all_gather.6 = f32[1024,16]{0,1:T(8,128)S(1)} all-gather(f32[128,16]{0,1:T(8,128)S(1)} %bitcast.76), channel_id=1, replica_groups=mesh['dp'=8,'var'=4] {'dp'}, dimensions={0}, use_global_device_ids=true | all-gather | bytes 73728 | tf_op jit(solution)/shard_map/all_gather | solution.py:40
  45.9 1.8 %bitcast_reduce_fusion = (f32[6,256]{1,0:T(8,128)S(1)}, f32[6,1024,256]{1,2,0:T(8,128)S(1)}) fusion(f32[6,1024]{1,0:T(8,128)S(1)} %convert_element_type.27, bf16[6,4,1024]{2,1,0:T(4,128)(2,1)S(1)} %gather_fusion, bf16[1,6,4,256]{3,2,1,0:T(4,128)(2,1)} %param.11), kind=kOutput, calls=%fused_computation.3 | convolution fusion | flops 15727104 | bytes 6383616 | tf_op jit(solution)/shard_map/skp,skd->spd/dot_general | solution.py:28
  47.8 0.0 copy-start.2
  47.8 0.0 copy-start.3
  47.8 1.0 multiply_reduce_fusion
  48.8 0.0 copy-done.2
  48.8 0.0 copy-done.3
  48.8 1.4 %add_convert_fusion = bf16[6,256,1024]{2,1,0:T(8,128)(2,1)S(1)} fusion(f32[6,1024,256]{1,2,0:T(8,128)S(1)} %get-tuple-element.10, f32[1024]{0:T(1024)S(1)} %copy-done.2, f32[1024]{0:T(1024)S(1)} %copy-done.3, f32[6,256]{1,0:T(8,128)S(1)} %add_rsqrt_fusion, f32[6,256]{1,0:T(8,128)S(1)} %broadcast_multiply_fusion, f32[6,1024]{1,0:T(8,128)S(1)} %convert_element_type.27), kind=kLoop, calls=%fused_computation.6 | loop fusion | flops 9437184 | bytes 9482240 | tf_op jit(solution)/shard_map/convert_element_type | solution.py:32
  50.2 0.0 copy-start.1
  50.3 1.7 %copy-done.1 = bf16[6,256,1024]{2,1,0:T(8,128)(2,1)} copy-done((bf16[6,256,1024]{2,1,0:T(8,128)(2,1)}, bf16[6,256,1024]{2,1,0:T(8,128)(2,1)S(1)}, u32[]{:S(2)}) %copy-start.1) | copy-done | bytes 3145752
  51.9 2.5 %convolution_multiply_fusion = f32[1536,16]{0,1:T(8,128)S(1)} fusion(bf16[1536,1024]{1,0:T(8,128)(2,1)S(1)} %bitcast.67, f32[1024,16]{0,1:T(8,128)S(1)} %all_gather.6), kind=kOutput, calls=%fused_computation.10 | convolution fusion | flops 302014464 | bytes 3309568 | tf_op jit(solution)/shard_map/dot_general | solution.py:46
  55.2 0.1 broadcast_select_fusion
  55.2 0.4 copy.22
  55.7 1.0 reshape.90
  56.7 3.3 %all-to-all-start = ((f32[4,1,6144]{2,1,0:T(1,128)}), f32[4,1,6144]{2,1,0:T(1,128)S(1)}, u32[]{:S(2)}, u32[]{:S(2)}) async-start(f32[4,1,6144]{2,1,0:T(1,128)} %reshape.90), calls=%async_computation | async-start | bytes 196608 | tf_op jit(solution)/shard_map/all_to_all | solution.py:62
  60.0 1.4 %all-gather.2.cloned.1.call-done = bf16[1024,1024]{1,0:T(8,128)(2,1)} async-done(((bf16[128,1024]{1,0:T(8,128)(2,1)}), bf16[1024,1024]{1,0:T(8,128)(2,1)}) %all-gather.2.cloned.1.call-update) | async-done | bytes 2097168 | tf_op jit(solution)/shard_map/all_gather | solution.py:43
  61.5 6.0 %convolution_convert_fusion = bf16[1536,1024]{1,0:T(8,128)(2,1)S(1)} fusion(bf16[1536,1024]{1,0:T(8,128)(2,1)} %bitcast.68, bf16[1024,1024]{1,0:T(8,128)(2,1)} %all-gather.2.cloned.1.call-done), kind=kOutput, calls=%fused_computation.8 | convolution fusion | flops 3222798336 | bytes 8388608 | tf_op jit(solution)/shard_map/dot_general | solution.py:41
  67.5 0.3 slice_bitcast_fusion.3
  67.8 1.9 %pad_maximum_fusion = bf16[4,6,64,1024]{3,2,1,0:T(8,128)(2,1)} fusion(bf16[1,6,64,1024]{3,2,1,0:T(8,128)(2,1)S(1)} %get-tuple-element.6, bf16[1,6,64,1024]{3,2,1,0:T(8,128)(2,1)S(1)} %get-tuple-element.7, bf16[1,6,64,1024]{3,2,1,0:T(8,128)(2,1)S(1)} %get-tuple-element.8, bf16[1,6,64,1024]{3,2,1,0:T(8,128)(2,1)S(1)} %get-tuple-element.5), kind=kLoop, calls=%fused_computation.9 | loop fusion | flops 4718592 | bytes 6291456 | tf_op jit(solution)/shard_map/stack | solution.py:56
  69.7 0.0 all-to-all-done
  69.7 4.8 %all-to-all-start.1 = ((bf16[4,6,64,1024]{3,2,1,0:T(8,128)(2,1)}), bf16[4,6,64,1024]{3,2,1,0:T(8,128)(2,1)}, u32[]{:S(2)}, u32[]{:S(2)}) async-start(bf16[4,6,64,1024]{3,2,1,0:T(8,128)(2,1)} %pad_maximum_fusion), calls=%async_computation.1 | async-start | bytes 6291456 | tf_op jit(solution)/shard_map/all_to_all | solution.py:55
  74.5 0.5 broadcast.67
  75.0 0.9 reduce.2
  75.9 0.5 reshape.91
  76.4 0.3 copy.31
  76.7 0.1 bitcast_reduce_fusion.1
  76.8 0.5 copy.28
  77.4 0.1 exponential_reduce_fusion
  77.5 0.1 copy.25
  77.6 33.7 %all-to-all-done.1 = bf16[4,6,64,1024]{3,2,1,0:T(8,128)(2,1)} async-done(((bf16[4,6,64,1024]{3,2,1,0:T(8,128)(2,1)}), bf16[4,6,64,1024]{3,2,1,0:T(8,128)(2,1)}, u32[]{:S(2)}, u32[]{:S(2)}) %all-to-all-start.1) | async-done | bytes 3145760 | tf_op jit(solution)/shard_map/all_to_all | solution.py:55
  111.3 9.2 %reshape_reshape.3 = bf16[24,64,16,64]{3,2,1,0:T(8,128)(2,1)} reshape(bf16[4,6,64,1024]{3,2,1,0:T(8,128)(2,1)} %all-to-all-done.1) | data formatting | bytes 6291456 | tf_op jit(solution)/shard_map/reshape;reshape | solution.py:70
  120.5 8.0 %fusion = f32[64,16,1,64]{3,2,1,0:T(1,128)S(1)} fusion(bf16[24,64,16,1]{0,3,2,1:T(2,128)(2,1)S(1)} %copy.28, bf16[24,64,16,64]{3,2,1,0:T(8,128)(2,1)} %reshape_reshape.3), kind=kOutput, calls=%fused_computation.4 | convolution fusion | flops 3145728 | bytes 3457024 | tf_op jit(solution)/shard_map/sph,sphe->phe/dot_general | solution.py:67
  128.4 0.2 divide_convert_fusion
  128.7 0.2 convert_element_type.32
  128.9 0.0 copy-done
  128.9 1.1 fusion.2
  (8 shorter events, 0.1 us)
Async XLA Ops:
  6.5 122.3 %copy-start = (bf16[1024,1024]{1,0:T(8,128)(2,1)S(1)}, bf16[1024,1024]{1,0:T(8,128)(2,1)}, u32[]{:S(2)}) copy-start(bf16[1024,1024]{1,0:T(8,128)(2,1)} %param.21) | copy-start | bytes 6291460
  6.5 54.9 %all-gather.2.cloned.1.call-start = ((), (), s32[]{:S(2)}) async-start(), calls=%async_computation.2 | async-start | bytes 2359296 | tf_op jit(solution)/shard_map/all_gather | solution.py:43
  47.8 1.0 copy-start.2
  47.8 1.0 copy-start.3
  50.2 1.7 %copy-start.1 = (bf16[6,256,1024]{2,1,0:T(8,128)(2,1)}, bf16[6,256,1024]{2,1,0:T(8,128)(2,1)S(1)}, u32[]{:S(2)}) copy-start(bf16[6,256,1024]{2,1,0:T(8,128)(2,1)S(1)} %add_convert_fusion) | copy-start | bytes 9437188
  56.7 13.0 %all-to-all-start = ((f32[4,1,6144]{2,1,0:T(1,128)}), f32[4,1,6144]{2,1,0:T(1,128)S(1)}, u32[]{:S(2)}, u32[]{:S(2)}) async-start(f32[4,1,6144]{2,1,0:T(1,128)} %reshape.90), calls=%async_computation | async-start | bytes 196608 | tf_op jit(solution)/shard_map/all_to_all | solution.py:62
  69.7 41.6 %all-to-all-start.1 = ((bf16[4,6,64,1024]{3,2,1,0:T(8,128)(2,1)}), bf16[4,6,64,1024]{3,2,1,0:T(8,128)(2,1)}, u32[]{:S(2)}, u32[]{:S(2)}) async-start(bf16[4,6,64,1024]{3,2,1,0:T(8,128)(2,1)} %pad_maximum_fusion), calls=%async_computation.1 | async-start | bytes 6291456 | tf_op jit(solution)/shard_map/all_to_all | solution.py:55
Sparse Core Ops, SparseCore 0:
  9.5 51.9 all-gather.1
